TPU v7x, 1024 devices: a whole 8x8x8 slice. The times are simulated.
1024 devices in a mesh: lat: 64 (over y_lo, x, core), lev: 16 (over y_hi, z).
Axes of the slice: x: 8, y: 8 (y_hi: 2, y_lo: 4; y = y_hi * 4 + y_lo), z: 8, core: 2. Of those that a mesh axis runs over, the one named last changes fastest.
Arguments:
- grid: bfloat16 [128, 1024, 2, 2, 8, 128], P(None, 'lat', None, None, None, 'lev'), may hold values from -6 to 6
- legendre: bfloat16 [128, 2, 1024, 512], P('lat'), may hold values from -0.1875 to 0.1875
- quad_weights: float32 [1024], P('lat'), may hold values from 0.25 to 4
- cycle_points: int32 [1024], P('lat'), may hold values from 20 to 4116, as said below
- wave_ids: int32 [128], replicated, may hold values from 0 to 1023, as said below
- mode_projection: bfloat16 [128, 128], replicated, may hold values from -0.5 to 0.5
- vertical_modes: bfloat16 [128, 128], replicated, may hold values from -0.5 to 0.5
- mode_rates: float32 [128], replicated, may hold values from 0.05 to 5
Outputs:
- grid_out: bfloat16 [128, 1024, 2, 2, 8, 128], P(None, 'lat', None, None, None, 'lev')
Inputs may be any that keep to these rules, and one draw needn't show every extreme that they name: `cycle_points`: nondecreasing from the first cycle pair to the last; the first cycle pair has the fewest points and the last the most. `wave_ids`: slots 2 i and 2 i + 1 carry wavenumbers m and 1023 - m; no wavenumber appears twice.
All inputs are finite; a program needn't handle non-finite values.
Results may differ from a plain program's by a relative error of at most 0.0073.
Values may be sent and summed in bfloat16 or wider, within the bound.
A program may use at most 64 MiB of HBM per device.

v0:
```python
import jax
import jax.numpy as jnp
from jax import lax
from jax.sharding import PartitionSpec as P

coupling = 2.0


def order_table(wave_local, k_count):
    parity = jnp.arange(2, dtype=jnp.int32)
    k_index = jnp.arange(k_count, dtype=jnp.int32)
    return wave_local[:, None, None] + parity[None, :, None] + 2 * k_index[None, None, :]


def forward_transform(legendre, values_in):
    return jnp.einsum("spjk,sjpc->spkc", legendre, values_in, preferred_element_type=jnp.float32)


def inverse_transform(legendre, coeffs):
    return jnp.einsum("spjk,spkc->sjpc", legendre, coeffs, preferred_element_type=jnp.float32)


def vertical_solve(spectral, growth, mode_projection, vertical_modes, mode_rates):
    level_dim = spectral.ndim - 1
    projected = lax.dot_general(
        spectral,
        mode_projection,
        (((level_dim,), (1,)), ((), ())),
        preferred_element_type=jnp.float32,
    )
    damped = (projected / (1.0 + growth * mode_rates)).astype(jnp.bfloat16)
    solved = lax.dot_general(
        damped, vertical_modes, (((level_dim,), (1,)), ((), ())), preferred_element_type=jnp.float32
    )
    return solved.astype(jnp.bfloat16)


def local(
    grid,
    legendre,
    quad_weights,
    cycle_points,
    wave_ids,
    mode_projection,
    vertical_modes,
    mode_rates,
):
    slot_count, cycle_local = (grid.shape[0], grid.shape[1])
    fields_count, levels_local = (grid.shape[4], grid.shape[5])
    per_device, cycles_all, k_half = (legendre.shape[0], legendre.shape[2], legendre.shape[3])
    mode_total = 2 * k_half
    levels_all = mode_projection.shape[0]
    present = (2 * wave_ids[:, None] < cycle_points[None, :]).astype(jnp.float32)
    weighting = (present * quad_weights[None, :])[:, :, None, None, None]
    north_cycle = grid[:, :, 0].astype(jnp.float32)
    south_cycle = grid[:, :, 1].astype(jnp.float32)
    even_part = (weighting * (north_cycle + south_cycle)).astype(jnp.bfloat16)
    odd_part = (weighting * (north_cycle - south_cycle)).astype(jnp.bfloat16)
    folded = jnp.stack([even_part, odd_part], axis=2)
    wave_local = lax.dynamic_slice_in_dim(wave_ids, lax.axis_index("lat") * per_device, per_device)
    full_order = order_table(wave_local, k_half)
    inside = (full_order <= mode_total - 1)[:, :, :, None]
    stacked = folded.reshape(slot_count, cycle_local, 2, 2 * fields_count, levels_local)
    gathered = lax.all_to_all(
        lax.all_to_all(stacked, "lat", split_axis=0, concat_axis=1, tiled=True),
        "lev",
        split_axis=3,
        concat_axis=4,
        tiled=True,
    )
    mixed_local = gathered.shape[3]
    values_in = gathered.reshape(per_device, cycles_all, 2, -1)
    spectral = jnp.where(inside, forward_transform(legendre, values_in), 0.0).astype(jnp.bfloat16)
    spectral = spectral.reshape(per_device, 2, k_half, mixed_local, levels_all)
    order_float = full_order.astype(jnp.float32)
    growth = (coupling * order_float * (order_float + 1.0) / (mode_total * mode_total))[
        :, :, :, None, None
    ]
    solved = vertical_solve(spectral, growth, mode_projection, vertical_modes, mode_rates)
    returned = inverse_transform(legendre, solved.reshape(per_device, 2, k_half, -1)).astype(
        jnp.bfloat16
    )
    returned = returned.reshape(per_device, cycles_all, 2, mixed_local, levels_all)
    unfolded = lax.all_to_all(
        lax.all_to_all(returned, "lat", split_axis=1, concat_axis=0, tiled=True),
        "lev",
        split_axis=4,
        concat_axis=3,
        tiled=True,
    )
    unfolded = unfolded.reshape(slot_count, cycle_local, 2, 2, fields_count, levels_local)
    even_back = unfolded[:, :, 0].astype(jnp.float32)
    odd_back = unfolded[:, :, 1].astype(jnp.float32)
    mask_cycles = present[:, :, None, None, None]
    north_out = mask_cycles * (even_back + odd_back)
    south_out = mask_cycles * (even_back - odd_back)
    return jnp.stack([north_out, south_out], axis=2).astype(jnp.bfloat16)


def solution(mesh):
    placed = (
        P(None, "lat", None, None, None, "lev"),
        P("lat", None, None, None),
        P("lat"),
        P("lat"),
        P(),
        P(),
        P(),
        P(),
    )
    return jax.shard_map(
        local,
        mesh=mesh,
        in_specs=placed,
        out_specs=P(None, "lat", None, None, None, "lev"),
        check_vma=False,
    )
```

profile of v0, /device:TPU:44, one launch (start us, length us, event | category | flops | bytes accessed | tf_op | source)
XLA Modules:
  0.0 248.7 jit_solution(16367851269155360345)
XLA Ops:
  0.0 0.7 broadcast_multiply_fusion
  0.7 0.7 compare_select_fusion
  1.4 1.6 fusion.5
  3.0 0.1 pad_maximum_fusion
  3.1 12.0 %copy.47 = bf16[128,16,2,16,8]{3,4,2,1,0:T(8,128)(2,1)} copy(bf16[128,16,2,16,8]{0,4,3,2,1:T(8,128)(2,1)S(1)} %pad_maximum_fusion) | data formatting | bytes 2097152 | tf_op jit(solution)/shard_map/stack | solution.py:59
  15.1 11.7 %reshape.146 = bf16[64,2,4096]{2,1,0:T(2,128)(2,1)S(1)} reshape(bf16[128,16,2,8,16]{4,3,2,1,0:T(8,128)(2,1)} %bitcast.43) | data formatting | bytes 2097152
  26.7 41.4 %all_to_all.54 = bf16[64,2,4096]{2,1,0:T(2,128)(2,1)S(1)} all-to-all(bf16[64,2,4096]{2,1,0:T(2,128)(2,1)S(1)} %reshape.146), channel_id=1, replica_groups=mesh['lat'=64,'lev'=16] {'lat'}, dimensions={0} | all-to-all | bytes 2097152 | tf_op jit(solution)/shard_map/all_to_all | solution.py:65
  68.2 7.5 %reshape.147 = bf16[128,16,2,8,16]{4,3,2,1,0:T(8,128)(2,1)} reshape(bf16[64,2,4096]{2,1,0:T(2,128)(2,1)S(1)} %all_to_all.54) | data formatting | bytes 2097152
  75.7 18.4 %copy.62 = bf16[2,64,16,2,16,8]{2,1,5,3,0,4:T(8,128)(2,1)} copy(bf16[2,64,16,2,16,8]{4,5,3,2,0,1:T(8,128)(2,1)} %bitcast.44) | data formatting | bytes 2097152 | tf_op jit(solution)/shard_map/all_to_all | solution.py:65
  94.1 15.8 %reshape.145 = bf16[2,1024,2,16,8]{1,4,2,0,3:T(8,128)(2,1)} reshape(bf16[2,64,16,2,16,8]{2,1,5,3,0,4:T(8,128)(2,1)} %copy.62) | data formatting | bytes 2097152 | tf_op jit(solution)/shard_map/all_to_all | solution.py:65
  110.0 14.3 %all-to-all-start.1 = ((bf16[2,1024,2,16,8]{1,4,2,0,3:T(8,128)(2,1)}), bf16[2,1024,2,16,8]{1,4,2,0,3:T(8,128)(2,1)S(1)}, u32[]{:S(2)}, u32[]{:S(2)}) async-start(bf16[2,1024,2,16,8]{1,4,2,0,3:T(8,128)(2,1)} %reshape.145), calls=%async_computation.1 | async-start | bytes 2097152 | tf_op jit(solution)/shard_map/all_to_all | solution.py:64
  124.3 0.1 dynamic_slice.3
  124.4 0.1 iota_add_fusion
  124.5 0.1 add_compare_fusion
  124.5 0.1 fusion.24
  124.6 35.5 %all-to-all-done.1 = bf16[2,1024,2,16,8]{1,4,2,0,3:T(8,128)(2,1)S(1)} async-done(((bf16[2,1024,2,16,8]{1,4,2,0,3:T(8,128)(2,1)}), bf16[2,1024,2,16,8]{1,4,2,0,3:T(8,128)(2,1)S(1)}, u32[]{:S(2)}, u32[]{:S(2)}) %all-to-all-start.1) | async-done | bytes 1048608 | tf_op jit(solution)/shard_map/all_to_all | solution.py:64
  160.1 0.0 copy-done.5
  160.1 3.2 %fusion.2 = bf16[2,2,512,128]{3,2,1,0:T(8,128)(2,1)S(1)} fusion(bf16[2,2,1024,512]{3,2,1,0:T(8,128)(2,1)} %param.9, bf16[2,1024,2,16,8]{1,4,2,0,3:T(8,128)(2,1)S(1)} %all-to-all-done.1, f32[128]{0:T(128)S(1)} %copy-done.5, f32[2,2,512]{2,1,0:T(2,128)S(1)} %fusion.24, pred[2,2,512]{2,1,0:T(4,128)(4,1)S(1)} %add_compare_fusion, bf16[128,128]{1,0:T(8,128)(2,1)S(1)} %copy-done.3), kind=kOutput, calls=%fused_computation.9 | convolution fusion | flops 605552640 | bytes 5810688 | tf_op jit(solution)/shard_map/dot_general | solution.py:25
  163.3 3.7 %fusion = bf16[2,1024,2,1,128]{1,4,2,0,3:T(8,128)(2,1)S(1)} fusion(bf16[2,2,1024,512]{3,2,1,0:T(8,128)(2,1)} %param.9, bf16[2,2,512,128]{3,2,1,0:T(8,128)(2,1)S(1)} %fusion.2, bf16[128,128]{1,0:T(8,128)(2,1)S(1)} %copy-done), kind=kOutput, calls=%fused_computation.1 | convolution fusion | flops 604766208 | bytes 5799936 | tf_op jit(solution)/shard_map/spjk,spkc->sjpc/dot_general | solution.py:20
  167.0 0.9 copy.53
  167.9 33.1 %all_to_all.55 = bf16[2,1024,2,1,128]{4,2,0,3,1:T(2,128)(2,1)S(1)} all-to-all(bf16[2,1024,2,1,128]{4,2,0,3,1:T(2,128)(2,1)S(1)} %copy.53), channel_id=1, replica_groups=mesh['lat'=64,'lev'=16] {'lat'}, dimensions={1} | all-to-all | bytes 2097152 | tf_op jit(solution)/shard_map/all_to_all | solution.py:85
  201.0 0.1 copy.54
  201.1 0.3 copy.55
  201.4 2.3 copy.56
  203.7 7.3 %all-to-all-start.3 = ((bf16[128,16,2,1,128]{0,1,3,2,4:T(8,128)(2,1)}), bf16[128,16,2,1,128]{0,1,3,2,4:T(8,128)(2,1)S(1)}, u32[]{:S(2)}, u32[]{:S(2)}) async-start(bf16[128,16,2,1,128]{0,1,3,2,4:T(8,128)(2,1)} %copy.56), calls=%async_computation.3 | async-start | bytes 2097152 | tf_op jit(solution)/shard_map/all_to_all | solution.py:84
  211.0 0.0 copy-done.1
  211.1 0.1 compare_convert_fusion
  211.1 35.7 %all-to-all-done.3 = bf16[128,16,2,1,128]{0,1,3,2,4:T(8,128)(2,1)S(1)} async-done(((bf16[128,16,2,1,128]{0,1,3,2,4:T(8,128)(2,1)}), bf16[128,16,2,1,128]{0,1,3,2,4:T(8,128)(2,1)S(1)}, u32[]{:S(2)}, u32[]{:S(2)}) %all-to-all-start.3) | async-done | bytes 1048608 | tf_op jit(solution)/shard_map/all_to_all | solution.py:84
  246.9 0.4 copy.57
  247.3 0.4 fusion.9
  247.7 0.0 copy-start.2
  247.7 1.0 copy-done.2
  (10 shorter events, 0.0 us)
Async XLA Ops:
  0.0 163.3 %copy-start = (bf16[128,128]{1,0:T(8,128)(2,1)S(1)}, bf16[128,128]{1,0:T(8,128)(2,1)}, u32[]{:S(2)}) copy-start(bf16[128,128]{1,0:T(8,128)(2,1)} %param.14) | copy-start | bytes 98308
  94.1 30.2 %copy-start.4 = (s32[128]{0:T(128)S(1)}, s32[128]{0:T(128)}, u32[]{:S(2)}) copy-start(s32[128]{0:T(128)} %param.12) | copy-start | bytes 1540
  94.1 66.0 %copy-start.3 = (bf16[128,128]{1,0:T(8,128)(2,1)S(1)}, bf16[128,128]{1,0:T(8,128)(2,1)}, u32[]{:S(2)}) copy-start(bf16[128,128]{1,0:T(8,128)(2,1)} %param.13) | copy-start | bytes 98308
  94.1 66.0 %copy-start.5 = (f32[128]{0:T(128)S(1)}, f32[128]{0:T(128)}, u32[]{:S(2)}) copy-start(f32[128]{0:T(128)} %param.15) | copy-start | bytes 1540
  110.0 50.1 %all-to-all-start.1 = ((bf16[2,1024,2,16,8]{1,4,2,0,3:T(8,128)(2,1)}), bf16[2,1024,2,16,8]{1,4,2,0,3:T(8,128)(2,1)S(1)}, u32[]{:S(2)}, u32[]{:S(2)}) async-start(bf16[2,1024,2,16,8]{1,4,2,0,3:T(8,128)(2,1)} %reshape.145), calls=%async_computation.1 | async-start | bytes 2097152 | tf_op jit(solution)/shard_map/all_to_all | solution.py:64
  201.0 10.1 %copy-start.1 = (s32[16]{0:T(128)S(1)}, s32[16]{0:T(128)}, u32[]{:S(2)}) copy-start(s32[16]{0:T(128)} %param.11) | copy-start | bytes 196
  203.7 43.2 %all-to-all-start.3 = ((bf16[128,16,2,1,128]{0,1,3,2,4:T(8,128)(2,1)}), bf16[128,16,2,1,128]{0,1,3,2,4:T(8,128)(2,1)S(1)}, u32[]{:S(2)}, u32[]{:S(2)}) async-start(bf16[128,16,2,1,128]{0,1,3,2,4:T(8,128)(2,1)} %copy.56), calls=%async_computation.3 | async-start | bytes 2097152 | tf_op jit(solution)/shard_map/all_to_all | solution.py:84
  247.7 1.0 copy-start.2
where the time goes:
time: 250 us; the launch traced here: 249 us
  blocking collectives  74.5 us (30%)
  waiting for transfers between devices  71.2 us (28%)
  local copies, waits for them, and re-layouts  70.4 us (28%)
  starting transfers between devices  21.6 us (9%)
  matrix products  6.9 us (3%)
  other arithmetic  3.82 us (2%)
    all_to_all x1, blocking collectives, local(): lax.all_to_all(stacked, 'lat', split_axis=0, concat_axis=1, tiled=True)  41.4 us
    all_to_all x1, waiting for transfers between devices, local(): lax.all_to_all(lax.all_to_all(returned, 'lat', split_axis=1, concat_axis=...  35.7 us
    all_to_all x1, waiting for transfers between devices, local(): lax.all_to_all(lax.all_to_all(stacked, 'lat', split_axis=0, concat_axis=1...  35.5 us
    all_to_all x2, local copies, waits for them, and re-layouts, local(): lax.all_to_all(stacked, 'lat', split_axis=0, concat_axis=1, tiled=True)  34.3 us
    all_to_all x1, blocking collectives, local(): lax.all_to_all(returned, 'lat', split_axis=1, concat_axis=0, tiled=True)  33.1 us
    unnamed x14, local copies, waits for them, and re-layouts  20.2 us
    all_to_all x1, starting transfers between devices, local(): lax.all_to_all(lax.all_to_all(stacked, 'lat', split_axis=0, concat_axis=1...  14.3 us
    another operation x1, local copies, waits for them, and re-layouts, local(): folded = jnp.stack([even_part, odd_part], axis=2)  12 us
  transfers between devices with their start and end apart: 2, of which 2 were waited for; matrix products, arithmetic and copies ran while one was open for 0% of the time, Pallas kernels for 0%

commit v1 on v0

v1 whole, which is shorter than its diff:
```python
import functools

import jax
import jax.numpy as jnp
from jax import lax
from jax.experimental import pallas as pl
from jax.experimental.pallas import tpu as pltpu
from jax.sharding import PartitionSpec as P

MESH = pl.DeviceIdType.MESH
coupling = 2.0
GROUP = 8
LANE_PAD = 128
F32 = jnp.float32
BF16 = jnp.bfloat16


def matmul(a, b):
    return lax.dot_general(a, b, (((1,), (0,)), ((), ())), preferred_element_type=F32)


def matmul_nt(a, b):
    return lax.dot_general(a, b, (((1,), (1,)), ((), ())), preferred_element_type=F32)


def iotas(shape):
    return lax.broadcasted_iota(jnp.int32, shape, 0), lax.broadcasted_iota(jnp.int32, shape, 1)


def unit(condition):
    return jnp.where(condition, 1.0, 0.0).astype(BF16)


def step_kernel(
    n_lat,
    n_lev,
    grid_ref,
    leg_hbm,
    quad_ref,
    cycle_ref,
    wave_ref,
    wave_row_ref,
    project_ref,
    modes_ref,
    rate_ref,
    out_ref,
    leg,
    turned,
    send,
    recv,
    pack_send_0,
    pack_send_1,
    pack_recv_0,
    pack_recv_1,
    solve_send_0,
    solve_send_1,
    solve_recv_0,
    solve_recv_1,
    back_send,
    back_recv,
    flip_0,
    flip_1,
    leg_sem,
    send_sem,
    recv_sem,
):
    lat, lev = lax.axis_index("lat"), lax.axis_index("lev")
    cycles, _, columns, slots = grid_ref.shape
    k_half = leg.shape[3]
    mode_total = 2 * k_half
    rows = cycles * GROUP
    groups = slots // GROUP
    levels = project_ref.shape[0]
    pack_send = (pack_send_0, pack_send_1)
    pack_recv = (pack_recv_0, pack_recv_1)
    solve_send = (solve_send_0, solve_send_1)
    solve_recv = (solve_recv_0, solve_recv_1)
    flips = (flip_0, flip_1)

    barrier = pltpu.get_barrier_semaphore()

    @pl.loop(1, n_lat)
    def _(r):
        pl.semaphore_signal(
            barrier, inc=1, device_id=(lax.rem(lat + r, n_lat), lev), device_id_type=MESH
        )

    @pl.loop(1, n_lev)
    def _(r):
        pl.semaphore_signal(
            barrier, inc=1, device_id=(lat, lax.rem(lev + r, n_lev)), device_id_type=MESH
        )

    leg_copy = pltpu.make_async_copy(leg_hbm, leg, leg_sem)
    leg_copy.start()

    row, col = iotas((columns, columns))
    eye_columns = unit(row == col)
    row, col = iotas((slots, slots))
    eye_slots = unit(row == col)
    row, col = iotas((rows, rows))
    spread = unit(col == (row % cycles) * GROUP + row // cycles)
    collect = unit(col == (row % GROUP) * cycles + row // GROUP)

    def exchange_lat(stage, p, source, target):
        @pl.loop(1, n_lat)
        def _(r):
            peer = lax.rem(lat + r, n_lat)
            pltpu.make_async_remote_copy(
                src_ref=source(peer),
                dst_ref=target(lat),
                send_sem=send_sem.at[stage, p],
                recv_sem=recv_sem.at[stage, p],
                device_id=(peer, lev),
                device_id_type=MESH,
            ).start()

    def exchange_lev(stage, p, source, target):
        @pl.loop(1, n_lev)
        def _(r):
            peer = lax.rem(lev + r, n_lev)
            pltpu.make_async_remote_copy(
                src_ref=source.at[peer],
                dst_ref=target.at[lev],
                send_sem=send_sem.at[stage, p],
                recv_sem=recv_sem.at[stage, p],
                device_id=(lat, peer),
                device_id_type=MESH,
            ).start()

    def wait_all(view, semaphore):
        pltpu.make_async_copy(view, view, semaphore).wait()

    def lat_view(p):
        return send.at[p, pl.ds(0, slots - 2)]

    def lev_view(p):
        return pack_send[p].at[pl.ds(0, n_lev - 1)]

    def own_rows(index):
        return pl.ds(pl.multiple_of(index * cycles, cycles), cycles)

    def fold(p):
        @pl.loop(0, cycles)
        def _(j):
            present = jnp.where(2 * wave_row_ref[...] < cycle_ref[j], quad_ref[j], 0.0)
            north = grid_ref[j, 0].astype(F32)
            south = grid_ref[j, 1].astype(F32)
            total = north + south if p == 0 else north - south
            turned[p, j] = matmul_nt(eye_slots, (present * total).astype(BF16))

        @pl.loop(0, groups)
        def _(g):
            block = turned[p, :, pl.ds(pl.multiple_of(g * GROUP, GROUP), GROUP), :]
            block = block.reshape(rows, columns).astype(BF16)
            moved = matmul(spread, block).astype(BF16)
            send[p, pl.ds(g * GROUP, GROUP)] = moved.reshape(GROUP, cycles, columns)

    def send_fold(p):
        exchange_lat(
            0,
            p,
            lambda peer: send.at[p, pl.ds(2 * peer, 2)],
            lambda me: recv.at[p, :, own_rows(me), :],
        )
        for slot in range(2):
            recv[p, slot, own_rows(lat), :] = send[p, 2 * lat + slot]

    def order(p, slot):
        k_index = lax.broadcasted_iota(jnp.int32, (1, k_half), 1)
        return wave_ref[2 * lat + slot] + p + 2 * k_index

    def forward(p):
        wait_all(lat_view(p), recv_sem.at[0, p])
        parts = []
        for slot in range(2):
            across = matmul_nt(eye_columns, recv[p, slot]).astype(BF16)
            spectral = matmul(across, leg[slot, p])
            parts.append(jnp.where(order(p, slot) <= mode_total - 1, spectral, 0.0))
        flipped = matmul(parts[1].astype(BF16), flips[p][...])
        packed = flipped[:, :k_half] + parts[0]
        pack_send[p][:, :, :k_half] = packed.reshape(n_lev, GROUP, k_half).astype(BF16)
        if flipped.shape[1] > k_half:
            rest = flipped[:, k_half:]
            pack_send[p][:, :, k_half:] = rest.reshape(n_lev, GROUP, -1).astype(BF16)
        exchange_lev(1, p, pack_send[p], pack_recv[p])
        pack_recv[p][lev] = pack_send[p][lev]

    def solve(p):
        wait_all(lev_view(p), recv_sem.at[1, p])
        packed = pack_recv[p][...].astype(F32).reshape(levels, -1).astype(BF16)
        width = packed.shape[1]
        q_index = lax.broadcasted_iota(jnp.int32, (1, width), 1)
        first = wave_ref[2 * lat] + p + 2 * q_index
        second = wave_ref[2 * lat + 1] + p + 2 * (k_half - p - q_index)
        total_order = jnp.where(first <= mode_total - 1, first, second).astype(F32)
        growth = coupling * total_order * (total_order + 1.0) / (mode_total * mode_total)
        rates = jnp.transpose(jnp.broadcast_to(rate_ref[...], (levels, levels)))[:, :1]
        projected = matmul(project_ref[...], packed)
        damped = (projected / (1.0 + growth * rates)).astype(BF16)
        solved = matmul(modes_ref[...], damped)
        solve_send[p][...] = solved.reshape(n_lev, GROUP, width).astype(BF16)
        exchange_lev(2, p, solve_send[p], solve_recv[p])
        solve_recv[p][lev] = solve_send[p][lev]

    def inverse(p):
        wait_all(lev_view(p), recv_sem.at[2, p])
        packed = solve_recv[p][...].astype(F32).reshape(columns, -1)
        unpacked = (packed[:, :k_half], matmul_nt(packed.astype(BF16), flips[p][...]))
        for slot in range(2):
            coeffs = jnp.where(order(p, slot) <= mode_total - 1, unpacked[slot], 0.0)
            back_send[p, slot] = matmul_nt(leg[slot, p], coeffs.astype(BF16)).astype(BF16)
        exchange_lat(
            3,
            p,
            lambda peer: back_send.at[p, :, own_rows(peer), :],
            lambda me: back_recv.at[p, pl.ds(2 * me, 2)],
        )
        for slot in range(2):
            back_recv[p, 2 * lat + slot] = back_send[p, slot, own_rows(lat), :]

    def spread_back(p):
        wait_all(lat_view(p), recv_sem.at[3, p])

        @pl.loop(0, groups)
        def _(g):
            block = back_recv[p, pl.ds(g * GROUP, GROUP)].reshape(rows, columns)
            moved = matmul(collect, block).reshape(cycles, GROUP, columns)
            turned[p, :, pl.ds(pl.multiple_of(g * GROUP, GROUP), GROUP), :] = moved

    def unfold():
        @pl.loop(0, cycles)
        def _(j):
            present = jnp.where(2 * wave_row_ref[...] < cycle_ref[j], 1.0, 0.0)
            even = matmul_nt(eye_columns, turned[0, j].astype(BF16))
            odd = matmul_nt(eye_columns, turned[1, j].astype(BF16))
            out_ref[j, 0] = (present * (even + odd)).astype(BF16)
            out_ref[j, 1] = (present * (even - odd)).astype(BF16)

    fold(0)
    pl.semaphore_wait(barrier, n_lat + n_lev - 2)
    send_fold(0)
    fold(1)
    send_fold(1)
    for p in range(2):
        row, col = iotas(flips[p].shape)
        flips[p][...] = unit(row + col == k_half - p)
    leg_copy.wait()
    forward(0)
    solve(0)
    inverse(0)
    forward(1)
    solve(1)
    inverse(1)
    spread_back(0)
    spread_back(1)
    unfold()
    for p in range(2):
        wait_all(lat_view(p), send_sem.at[0, p])
        wait_all(lev_view(p), send_sem.at[1, p])
        wait_all(lev_view(p), send_sem.at[2, p])
        wait_all(lat_view(p), send_sem.at[3, p])


def local(
    n_lat,
    n_lev,
    grid,
    legendre,
    quad_weights,
    cycle_points,
    wave_ids,
    mode_projection,
    vertical_modes,
    mode_rates,
):
    slots, cycles, _, parts, fields, levels_local = grid.shape
    columns = parts * fields * levels_local
    k_half = legendre.shape[3]
    widths = (k_half + LANE_PAD, k_half)
    held = jnp.transpose(grid, (1, 2, 3, 4, 5, 0)).reshape(cycles, 2, columns, slots)
    vmem = pl.BlockSpec(memory_space=pltpu.VMEM)
    smem = pl.BlockSpec(memory_space=pltpu.SMEM)
    packs = [pltpu.VMEM((n_lev, GROUP, width), BF16) for width in widths]
    out = pl.pallas_call(
        functools.partial(step_kernel, n_lat, n_lev),
        out_shape=jax.ShapeDtypeStruct((cycles, 2, columns, slots), BF16),
        in_specs=[vmem, pl.BlockSpec(memory_space=pl.ANY), smem, smem, smem, vmem, vmem, vmem, vmem],
        out_specs=vmem,
        scratch_shapes=[
            pltpu.VMEM(legendre.shape, BF16),
            pltpu.VMEM((2, cycles, slots, columns), F32),
            pltpu.VMEM((2, slots, cycles, columns), BF16),
            pltpu.VMEM((2, 2, n_lat * cycles, columns), BF16),
            *packs,
            *packs,
            *packs,
            *packs,
            pltpu.VMEM((2, 2, n_lat * cycles, columns), BF16),
            pltpu.VMEM((2, slots, cycles, columns), BF16),
            *[pltpu.VMEM((k_half, width), BF16) for width in widths],
            pltpu.SemaphoreType.DMA,
            pltpu.SemaphoreType.DMA((4, 2)),
            pltpu.SemaphoreType.DMA((4, 2)),
        ],
        compiler_params=pltpu.CompilerParams(
            collective_id=0, has_side_effects=True, vmem_limit_bytes=48 * 1024 * 1024
        ),
        name="spectral_step",
    )(
        held,
        legendre,
        quad_weights,
        cycle_points,
        wave_ids,
        wave_ids.reshape(1, slots),
        mode_projection,
        vertical_modes,
        mode_rates.reshape(1, -1),
    )
    out = out.reshape(cycles, 2, parts, fields, levels_local, slots)
    return jnp.transpose(out, (5, 0, 1, 2, 3, 4))


def solution(mesh):
    placed = (
        P(None, "lat", None, None, None, "lev"),
        P("lat", None, None, None),
        P("lat"),
        P("lat"),
        P(),
        P(),
        P(),
        P(),
    )
    return jax.shard_map(
        functools.partial(local, mesh.shape["lat"], mesh.shape["lev"]),
        mesh=mesh,
        in_specs=placed,
        out_specs=P(None, "lat", None, None, None, "lev"),
        check_vma=False,
    )
```

time: 250 us -> 120 us (0.48)
  the two profiles are of different devices: /device:TPU:44 before, /device:TPU:1 now
where the time goes in v1:
time: 120 us; the launch traced here: 119 us
  Pallas kernels  113 us (94%)
  local copies, waits for them, and re-layouts  6.33 us (5%)
    pallas_call x1, Pallas kernels, local(): pl.pallas_call(functools.partial(step_kernel, n_lat, n_lev), out_shape=ja...  113 us
    unnamed x15, local copies, waits for them, and re-layouts  6.33 us

profile of v1, /device:TPU:1, one launch (start us, length us, event | category | flops | bytes accessed | tf_op | source)
XLA Modules:
  0.0 119.2 jit_solution(1503730079336737937)
XLA Ops:
  0.0 0.0 copy-start
  0.0 1.2 %copy-done = bf16[128,16,2,2,8,8]{0,5,4,3,2,1:T(8,128)(2,1)S(1)} copy-done((bf16[128,16,2,2,8,8]{0,5,4,3,2,1:T(8,128)(2,1)S(1)}, bf16[128,16,2,2,8,8]{0,5,4,3,2,1:T(8,128)(2,1)}, u32[]{:S(2)}) %copy-start) | copy-done | bytes 1048600
  1.2 0.0 copy-start.1
  1.2 0.8 copy-done.1
  2.0 0.0 copy-start.2
  2.0 0.8 copy-done.2
  2.7 0.0 copy-start.3
  2.7 0.7 copy-done.3
  3.4 0.0 copy-start.4
  3.4 0.7 copy-done.4
  4.1 0.0 copy-start.5
  4.1 0.7 copy-done.5
  4.7 0.0 copy-start.6
  4.7 0.7 copy-done.6
  5.4 112.8 %spectral_step.1 = bf16[16,2,128,128]{3,2,1,0:T(8,128)(2,1)S(1)} custom-call(bf16[16,2,128,128]{3,2,1,0:T(8,128)(2,1)S(1)} %bitcast.9, bf16[2,2,1024,512]{3,2,1,0:T(8,128)(2,1)} %leg_hbm.1, f32[16]{0:T(128)S(1)} %copy-done.4, s32[16]{0:T(128)S(1)} %copy-done.5, s32[128]{0:T(128)S(1)} %copy-done.3, s32[1,128]{1,0:T(1,128)S(1)} %bitcast.10, ...), custom_call_target="tpu_custom_call" | custom-call | tf_op jit(solution)/shard_map/spectral_step/pallas_call | solution.py:285
  118.2 1.0 copy.10
Async XLA Ops:
  0.0 1.2 %copy-start = (bf16[128,16,2,2,8,8]{0,5,4,3,2,1:T(8,128)(2,1)S(1)}, bf16[128,16,2,2,8,8]{0,5,4,3,2,1:T(8,128)(2,1)}, u32[]{:S(2)}) copy-start(bf16[128,16,2,2,8,8]{0,5,4,3,2,1:T(8,128)(2,1)} %param.8) | copy-start | bytes 3145732
  1.2 0.8 copy-start.1
  2.0 0.8 copy-start.2
  2.7 0.7 copy-start.3
  3.4 0.7 copy-start.4
  4.1 0.7 copy-start.5
  4.7 0.7 copy-start.6

commit v2 on v1

--- a/solution.py
+++ b/solution.py
@@ -34,8 +34,18 @@
 def step_kernel(
     n_lat,
     n_lev,
+    grid_hbm,
+    leg_hbm,
+    quad_hbm,
+    cycle_hbm,
+    wave_hbm,
+    wave_row_hbm,
+    project_hbm,
+    modes_hbm,
+    rate_hbm,
+    out_hbm,
     grid_ref,
-    leg_hbm,
+    leg,
     quad_ref,
     cycle_ref,
     wave_ref,
@@ -43,9 +53,8 @@
     project_ref,
     modes_ref,
     rate_ref,
-    out_ref,
-    leg,
     turned,
+    even_ref,
     send,
     recv,
     pack_send_0,
@@ -60,12 +69,13 @@
     back_recv,
     flip_0,
     flip_1,
-    leg_sem,
+    grid_sem,
+    input_sem,
     send_sem,
     recv_sem,
 ):
     lat, lev = lax.axis_index("lat"), lax.axis_index("lev")
-    cycles, _, columns, slots = grid_ref.shape
+    cycles, _, columns, slots = grid_hbm.shape
     k_half = leg.shape[3]
     mode_total = 2 * k_half
     rows = cycles * GROUP
@@ -77,6 +87,33 @@
     solve_recv = (solve_recv_0, solve_recv_1)
     flips = (flip_0, flip_1)
 
+    def grid_copy(j):
+        return pltpu.make_async_copy(grid_hbm.at[j], grid_ref.at[j], grid_sem.at[j])
+
+    inputs = [
+        (wave_row_hbm, wave_row_ref),
+        (cycle_hbm, cycle_ref),
+        (quad_hbm, quad_ref),
+        (wave_hbm, wave_ref),
+        (leg_hbm, leg),
+        (project_hbm, project_ref),
+        (modes_hbm, modes_ref),
+        (rate_hbm, rate_ref),
+    ]
+    copies = [
+        pltpu.make_async_copy(source, target, input_sem.at[i])
+        for i, (source, target) in enumerate(inputs)
+    ]
+    for copy in copies[:3]:
+        copy.start()
+
+    @pl.loop(0, cycles)
+    def _(j):
+        grid_copy(j).start()
+
+    for copy in copies[3:]:
+        copy.start()
+
     barrier = pltpu.get_barrier_semaphore()
 
     @pl.loop(1, n_lat)
@@ -91,8 +128,6 @@
             barrier, inc=1, device_id=(lat, lax.rem(lev + r, n_lev)), device_id_type=MESH
         )
 
-    leg_copy = pltpu.make_async_copy(leg_hbm, leg, leg_sem)
-    leg_copy.start()
 
     row, col = iotas((columns, columns))
     eye_columns = unit(row == col)
@@ -102,18 +137,27 @@
     spread = unit(col == (row % cycles) * GROUP + row // cycles)
     collect = unit(col == (row % GROUP) * cycles + row // GROUP)
 
+    x_size = min(8, n_lat // 2)
+    y_size = n_lat // (2 * x_size)
+    at_core, at_x, at_y = lax.rem(lat, 2), lax.rem(lat // 2, x_size), lat // (2 * x_size)
+    shifts = sorted(range(x_size), key=lambda d: -min(d, x_size - d))
+
     def exchange_lat(stage, p, source, target):
-        @pl.loop(1, n_lat)
-        def _(r):
-            peer = lax.rem(lat + r, n_lat)
-            pltpu.make_async_remote_copy(
-                src_ref=source(peer),
-                dst_ref=target(lat),
-                send_sem=send_sem.at[stage, p],
-                recv_sem=recv_sem.at[stage, p],
-                device_id=(peer, lev),
-                device_id_type=MESH,
-            ).start()
+        for shift in shifts:
+            to_x = lax.rem(at_x + shift, x_size)
+
+            @pl.loop(0 if shift else 1, 2 * y_size)
+            def _(t):
+                to_y = lax.rem(at_y + t // 2, y_size)
+                peer = (to_y * x_size + to_x) * 2 + lax.rem(at_core + t, 2)
+                pltpu.make_async_remote_copy(
+                    src_ref=source(peer),
+                    dst_ref=target(lat),
+                    send_sem=send_sem.at[stage, p],
+                    recv_sem=recv_sem.at[stage, p],
+                    device_id=(peer, lev),
+                    device_id_type=MESH,
+                ).start()
 
     def exchange_lev(stage, p, source, target):
         @pl.loop(1, n_lev)
@@ -141,15 +185,17 @@
         return pl.ds(pl.multiple_of(index * cycles, cycles), cycles)
 
     def fold(p):
-        @pl.loop(0, cycles)
+        @pl.loop(0, cycles, unroll=4)
         def _(j):
+            if p == 0:
+                grid_copy(j).wait()
             present = jnp.where(2 * wave_row_ref[...] < cycle_ref[j], quad_ref[j], 0.0)
             north = grid_ref[j, 0].astype(F32)
             south = grid_ref[j, 1].astype(F32)
             total = north + south if p == 0 else north - south
             turned[p, j] = matmul_nt(eye_slots, (present * total).astype(BF16))
 
-        @pl.loop(0, groups)
+        @pl.loop(0, groups, unroll=4)
         def _(g):
             block = turned[p, :, pl.ds(pl.multiple_of(g * GROUP, GROUP), GROUP), :]
             block = block.reshape(rows, columns).astype(BF16)
@@ -222,21 +268,34 @@
     def spread_back(p):
         wait_all(lat_view(p), recv_sem.at[3, p])
 
-        @pl.loop(0, groups)
+        @pl.loop(0, groups, unroll=4)
         def _(g):
             block = back_recv[p, pl.ds(g * GROUP, GROUP)].reshape(rows, columns)
             moved = matmul(collect, block).reshape(cycles, GROUP, columns)
             turned[p, :, pl.ds(pl.multiple_of(g * GROUP, GROUP), GROUP), :] = moved
 
+    def cross(p, j):
+        return matmul_nt(eye_columns, turned[p, j].astype(BF16))
+
+    def out_copy(j):
+        return pltpu.make_async_copy(grid_ref.at[j], out_hbm.at[j], grid_sem.at[j])
+
+    def turn_even():
+        @pl.loop(0, cycles, unroll=4)
+        def _(j):
+            even_ref[j] = cross(0, j)
+
     def unfold():
-        @pl.loop(0, cycles)
+        @pl.loop(0, cycles, unroll=4)
         def _(j):
             present = jnp.where(2 * wave_row_ref[...] < cycle_ref[j], 1.0, 0.0)
-            even = matmul_nt(eye_columns, turned[0, j].astype(BF16))
-            odd = matmul_nt(eye_columns, turned[1, j].astype(BF16))
-            out_ref[j, 0] = (present * (even + odd)).astype(BF16)
-            out_ref[j, 1] = (present * (even - odd)).astype(BF16)
-
+            even, odd = even_ref[j], cross(1, j)
+            grid_ref[j, 0] = (present * (even + odd)).astype(BF16)
+            grid_ref[j, 1] = (present * (even - odd)).astype(BF16)
+            out_copy(j).start()
+
+    for copy in copies[:3]:
+        copy.wait()
     fold(0)
     pl.semaphore_wait(barrier, n_lat + n_lev - 2)
     send_fold(0)
@@ -245,14 +304,16 @@
     for p in range(2):
         row, col = iotas(flips[p].shape)
         flips[p][...] = unit(row + col == k_half - p)
-    leg_copy.wait()
+    for copy in copies[3:]:
+        copy.wait()
     forward(0)
     solve(0)
+    forward(1)
     inverse(0)
-    forward(1)
     solve(1)
     inverse(1)
     spread_back(0)
+    turn_even()
     spread_back(1)
     unfold()
     for p in range(2):
@@ -260,6 +321,10 @@
         wait_all(lev_view(p), send_sem.at[1, p])
         wait_all(lev_view(p), send_sem.at[2, p])
         wait_all(lat_view(p), send_sem.at[3, p])
+
+    @pl.loop(0, cycles)
+    def _(j):
+        out_copy(j).wait()
 
 
 def local(
@@ -279,17 +344,25 @@
     k_half = legendre.shape[3]
     widths = (k_half + LANE_PAD, k_half)
     held = jnp.transpose(grid, (1, 2, 3, 4, 5, 0)).reshape(cycles, 2, columns, slots)
-    vmem = pl.BlockSpec(memory_space=pltpu.VMEM)
-    smem = pl.BlockSpec(memory_space=pltpu.SMEM)
+    hbm = pl.BlockSpec(memory_space=pltpu.HBM)
     packs = [pltpu.VMEM((n_lev, GROUP, width), BF16) for width in widths]
     out = pl.pallas_call(
         functools.partial(step_kernel, n_lat, n_lev),
         out_shape=jax.ShapeDtypeStruct((cycles, 2, columns, slots), BF16),
-        in_specs=[vmem, pl.BlockSpec(memory_space=pl.ANY), smem, smem, smem, vmem, vmem, vmem, vmem],
-        out_specs=vmem,
+        in_specs=[hbm] * 9,
+        out_specs=hbm,
         scratch_shapes=[
+            pltpu.VMEM(held.shape, BF16),
             pltpu.VMEM(legendre.shape, BF16),
+            pltpu.SMEM(quad_weights.shape, F32),
+            pltpu.SMEM(cycle_points.shape, jnp.int32),
+            pltpu.SMEM(wave_ids.shape, jnp.int32),
+            pltpu.VMEM((1, slots), jnp.int32),
+            pltpu.VMEM(mode_projection.shape, BF16),
+            pltpu.VMEM(vertical_modes.shape, BF16),
+            pltpu.VMEM((1, mode_rates.shape[0]), F32),
             pltpu.VMEM((2, cycles, slots, columns), F32),
+            pltpu.VMEM((cycles, columns, slots), F32),
             pltpu.VMEM((2, slots, cycles, columns), BF16),
             pltpu.VMEM((2, 2, n_lat * cycles, columns), BF16),
             *packs,
@@ -299,12 +372,13 @@
             pltpu.VMEM((2, 2, n_lat * cycles, columns), BF16),
             pltpu.VMEM((2, slots, cycles, columns), BF16),
             *[pltpu.VMEM((k_half, width), BF16) for width in widths],
-            pltpu.SemaphoreType.DMA,
+            pltpu.SemaphoreType.DMA((cycles,)),
+            pltpu.SemaphoreType.DMA((8,)),
             pltpu.SemaphoreType.DMA((4, 2)),
             pltpu.SemaphoreType.DMA((4, 2)),
         ],
         compiler_params=pltpu.CompilerParams(
-            collective_id=0, has_side_effects=True, vmem_limit_bytes=48 * 1024 * 1024
+            collective_id=0, has_side_effects=True, vmem_limit_bytes=62914560
         ),
         name="spectral_step",
     )(

time: 120 us -> 105 us (0.88)
  Pallas kernels: 113 us -> 103 us
  local copies, waits for them, and re-layouts: 6.33 us -> 2.31 us
    pallas_call x1, Pallas kernels: 113 us -> 103 us  [local(): pl.pallas_call(functools.partial(step_kernel, n_lat, n_lev), out_shape=ja...]
    unnamed x15 -> x1, local copies, waits for them, and re-layouts: 6.33 us -> 2.31 us
where the time goes in v2:
time: 105 us
  Pallas kernels  103 us (98%)
  local copies, waits for them, and re-layouts  2.31 us (2%)
    pallas_call x1, Pallas kernels, local(): pl.pallas_call(functools.partial(step_kernel, n_lat, n_lev), out_shape=ja...  103 us
    unnamed x1, local copies, waits for them, and re-layouts  2.31 us

profile of v2, /device:TPU:1, one launch (start us, length us, event | category | flops | bytes accessed | tf_op | source)
XLA Modules:
  0.0 105.1 jit_solution(8381716530757901540)
XLA Ops:
  0.0 102.7 %spectral_step.1 = bf16[16,2,128,128]{3,2,1,0:T(8,128)(2,1)} custom-call(bf16[16,2,128,128]{3,2,1,0:T(8,128)(2,1)} %bitcast.9, bf16[2,2,1024,512]{3,2,1,0:T(8,128)(2,1)} %leg_hbm.1, f32[16]{0:T(128)} %quad_hbm.1, s32[16]{0:T(128)} %cycle_hbm.1, s32[128]{0:T(128)} %wave_hbm.1, s32[1,128]{1,0:T(1,128)} %bitcast.10, bf16[128,128]{1,0:T(8,128)(2,1)} %project_hbm.1, ...), custom_call_target="tpu_custom_call" | custom-call | tf_op jit(solution)/shard_map/spectral_step/pallas_call | solution.py:349
  102.8 2.3 %copy.10 = bf16[128,16,2,2,8,8]{0,5,4,3,2,1:T(8,128)(2,1)} copy(bf16[128,16,2,2,8,8]{0,5,4,3,2,1:T(8,128)(2,1)} %bitcast.8) | data formatting | bytes 2097152

commit v3 on v2

--- a/solution.py
+++ b/solution.py
@@ -140,9 +140,14 @@
     x_size = min(8, n_lat // 2)
     y_size = n_lat // (2 * x_size)
     at_core, at_x, at_y = lax.rem(lat, 2), lax.rem(lat // 2, x_size), lat // (2 * x_size)
-    shifts = sorted(range(x_size), key=lambda d: -min(d, x_size - d))
-
-    def exchange_lat(stage, p, source, target):
+    near_last = sorted(range(x_size), key=lambda d: -min(d, x_size - d))
+    if x_size == 8:
+        split_forward = ((3, 5, 2, 6), (4, 1, 7, 0))
+        split_return = ((3, 5), (4, 2, 6, 1, 7, 0))
+    else:
+        split_forward = split_return = (near_last[:-1], near_last[-1:])
+
+    def exchange_lat(stage, p, shifts, source, target):
         for shift in shifts:
             to_x = lax.rem(at_x + shift, x_size)
 
@@ -159,10 +164,14 @@
                     device_id_type=MESH,
                 ).start()
 
+    z_size = n_lev // 2
+    at_z, at_half = lax.rem(lev, z_size), lev // z_size
+    hops = sorted(range(z_size), key=lambda d: -min(d, z_size - d))
+    lev_steps = [(half, hop) for half in (1, 0) for hop in hops if half or hop]
+
     def exchange_lev(stage, p, source, target):
-        @pl.loop(1, n_lev)
-        def _(r):
-            peer = lax.rem(lev + r, n_lev)
+        for half, hop in lev_steps:
+            peer = lax.rem(at_half + half, 2) * z_size + lax.rem(at_z + hop, z_size)
             pltpu.make_async_remote_copy(
                 src_ref=source.at[peer],
                 dst_ref=target.at[lev],
@@ -202,13 +211,16 @@
             moved = matmul(spread, block).astype(BF16)
             send[p, pl.ds(g * GROUP, GROUP)] = moved.reshape(GROUP, cycles, columns)
 
-    def send_fold(p):
+    def send_fold(p, shifts):
         exchange_lat(
             0,
             p,
+            shifts,
             lambda peer: send.at[p, pl.ds(2 * peer, 2)],
             lambda me: recv.at[p, :, own_rows(me), :],
         )
+
+    def keep_fold(p):
         for slot in range(2):
             recv[p, slot, own_rows(lat), :] = send[p, 2 * lat + slot]
 
@@ -256,12 +268,17 @@
         for slot in range(2):
             coeffs = jnp.where(order(p, slot) <= mode_total - 1, unpacked[slot], 0.0)
             back_send[p, slot] = matmul_nt(leg[slot, p], coeffs.astype(BF16)).astype(BF16)
+
+    def send_back(p, shifts):
         exchange_lat(
             3,
             p,
+            shifts,
             lambda peer: back_send.at[p, :, own_rows(peer), :],
             lambda me: back_recv.at[p, pl.ds(2 * me, 2)],
         )
+
+    def keep_back(p):
         for slot in range(2):
             back_recv[p, 2 * lat + slot] = back_send[p, slot, own_rows(lat), :]
 
@@ -298,20 +315,28 @@
         copy.wait()
     fold(0)
     pl.semaphore_wait(barrier, n_lat + n_lev - 2)
-    send_fold(0)
+    send_fold(0, near_last)
+    keep_fold(0)
     fold(1)
-    send_fold(1)
+    send_fold(1, split_forward[0])
+    keep_fold(1)
     for p in range(2):
         row, col = iotas(flips[p].shape)
         flips[p][...] = unit(row + col == k_half - p)
     for copy in copies[3:]:
         copy.wait()
     forward(0)
+    send_fold(1, split_forward[1])
     solve(0)
     forward(1)
     inverse(0)
+    send_back(0, split_return[0])
+    keep_back(0)
     solve(1)
+    send_back(0, split_return[1])
     inverse(1)
+    send_back(1, near_last)
+    keep_back(1)
     spread_back(0)
     turn_even()
     spread_back(1)

time: 105 us -> 98.9 us (0.942)
  Pallas kernels: 103 us -> 96.4 us
    pallas_call x1, Pallas kernels: 103 us -> 96.4 us  [local(): pl.pallas_call(functools.partial(step_kernel, n_lat, n_lev), out_shape=ja...]
where the time goes in v3:
time: 98.9 us; the launch traced here: 98.7 us
  Pallas kernels  96.4 us (97%)
  local copies, waits for them, and re-layouts  2.31 us (2%)
    pallas_call x1, Pallas kernels, local(): pl.pallas_call(functools.partial(step_kernel, n_lat, n_lev), out_shape=ja...  96.4 us
    unnamed x1, local copies, waits for them, and re-layouts  2.31 us

profile of v3, /device:TPU:1, one launch (start us, length us, event | category | flops | bytes accessed | tf_op | source)
XLA Modules:
  0.0 98.7 jit_solution(7695102117958640050)
XLA Ops:
  0.0 96.4 %spectral_step.1 = bf16[16,2,128,128]{3,2,1,0:T(8,128)(2,1)} custom-call(bf16[16,2,128,128]{3,2,1,0:T(8,128)(2,1)} %bitcast.9, bf16[2,2,1024,512]{3,2,1,0:T(8,128)(2,1)} %leg_hbm.1, f32[16]{0:T(128)} %quad_hbm.1, s32[16]{0:T(128)} %cycle_hbm.1, s32[128]{0:T(128)} %wave_hbm.1, s32[1,128]{1,0:T(1,128)} %bitcast.10, bf16[128,128]{1,0:T(8,128)(2,1)} %project_hbm.1, ...), custom_call_target="tpu_custom_call" | custom-call | tf_op jit(solution)/shard_map/spectral_step/pallas_call | solution.py:374
  96.4 2.3 %copy.10 = bf16[128,16,2,2,8,8]{0,5,4,3,2,1:T(8,128)(2,1)} copy(bf16[128,16,2,2,8,8]{0,5,4,3,2,1:T(8,128)(2,1)} %bitcast.8) | data formatting | bytes 2097152

commit v4 on v3

--- a/solution.py
+++ b/solution.py
@@ -142,7 +142,7 @@
     at_core, at_x, at_y = lax.rem(lat, 2), lax.rem(lat // 2, x_size), lat // (2 * x_size)
     near_last = sorted(range(x_size), key=lambda d: -min(d, x_size - d))
     if x_size == 8:
-        split_forward = ((3, 5, 2, 6), (4, 1, 7, 0))
+        split_forward = ((3, 5, 2, 6, 1), (4, 7, 0))
         split_return = ((3, 5), (4, 2, 6, 1, 7, 0))
     else:
         split_forward = split_return = (near_last[:-1], near_last[-1:])

time: 98.9 us -> 97.8 us (0.989)
  Pallas kernels: 96.4 us -> 95.3 us
    pallas_call x1, Pallas kernels: 96.4 us -> 95.3 us  [local(): pl.pallas_call(functools.partial(step_kernel, n_lat, n_lev), out_shape=ja...]
where the time goes in v4:
time: 97.8 us; the launch traced here: 97.6 us
  Pallas kernels  95.3 us (97%)
  local copies, waits for them, and re-layouts  2.31 us (2%)
    pallas_call x1, Pallas kernels, local(): pl.pallas_call(functools.partial(step_kernel, n_lat, n_lev), out_shape=ja...  95.3 us
    unnamed x1, local copies, waits for them, and re-layouts  2.31 us

profile of v4, /device:TPU:1, one launch (start us, length us, event | category | flops | bytes accessed | tf_op | source)
XLA Modules:
  0.0 97.6 jit_solution(4968706626428204701)
XLA Ops:
  0.0 95.3 %spectral_step.1 = bf16[16,2,128,128]{3,2,1,0:T(8,128)(2,1)} custom-call(bf16[16,2,128,128]{3,2,1,0:T(8,128)(2,1)} %bitcast.9, bf16[2,2,1024,512]{3,2,1,0:T(8,128)(2,1)} %leg_hbm.1, f32[16]{0:T(128)} %quad_hbm.1, s32[16]{0:T(128)} %cycle_hbm.1, s32[128]{0:T(128)} %wave_hbm.1, s32[1,128]{1,0:T(1,128)} %bitcast.10, bf16[128,128]{1,0:T(8,128)(2,1)} %project_hbm.1, ...), custom_call_target="tpu_custom_call" | custom-call | tf_op jit(solution)/shard_map/spectral_step/pallas_call | solution.py:374
  95.3 2.3 %copy.10 = bf16[128,16,2,2,8,8]{0,5,4,3,2,1:T(8,128)(2,1)} copy(bf16[128,16,2,2,8,8]{0,5,4,3,2,1:T(8,128)(2,1)} %bitcast.8) | data formatting | bytes 2097152
